TPU v7x, 256 devices: a whole 4x4x8 slice. The times are simulated.
256 devices in a mesh: frames: 8 (over x, core), codes: 32 (over y, z).
Axes of the slice: x: 4, y: 4, z: 8, core: 2. Of those that a mesh axis runs over, the one named last changes fastest.
Arguments:
- hidden: bfloat16 [32768, 1024], P('frames'), may hold values from -5 to 5
- head: bfloat16 [1024, 8192], P('frames', 'codes'), may hold values from -2 to 2
- chosen: int32 [8, 32768], P(None, 'frames'), may hold values from 0 to 1023
Outputs:
- confidence: float32 [8, 32768], P(None, 'frames')
- entropy: float32 [8, 32768], P(None, 'frames')
All inputs are finite; a program needn't handle non-finite values.
Results may differ from a plain program's by a relative error of at most 0.0003.
Values may be sent and summed in bfloat16 or wider, within the bound.
A program may use at most 64 MiB of HBM per device.

v0:
```python
import jax
import jax.numpy as jnp
from jax import lax
from jax.sharding import PartitionSpec as P

CODES = 1024


def from_everyone(x, axis):
    count = lax.axis_size(axis)
    return lax.all_to_all(jnp.broadcast_to(x[None], (count, *x.shape)), axis, 0, 0, tiled=True)


def laid_out(parts, dim):
    dims = list(parts.shape[1:])
    dims[dim] *= parts.shape[0]
    return jnp.moveaxis(parts, 0, dim).reshape(dims)


def collect(x, axis, dim):
    parts = from_everyone(x, axis)
    return laid_out(parts, dim)


def partner(block, axis, bit):
    count = lax.axis_size(axis)
    route = []
    for low in range(count):
        high = low | 1 << bit
        if high != low and high < count:
            route += [(low, high), (high, low)]
    return lax.ppermute(block, axis, route)


def gather_together(arrays, axis, dims):
    line = jnp.concatenate([a.reshape(-1) for a in arrays])
    lines, at, outs = (lax.all_gather(line, axis), 0, [])
    for a, dim in zip(arrays, dims):
        parts = lines[:, at : at + a.size].reshape(-1, *a.shape)
        outs.append(laid_out(parts, dim))
        at += a.size
    return tuple(outs)


def finish(top_score, exp_total, exp_logit, picked):
    log_total = top_score + jnp.log(exp_total)
    return (picked - log_total, log_total - exp_logit / exp_total)


def combine(earlier, later):
    highest = jnp.maximum(earlier[0], later[0])
    early_factor = jnp.exp(earlier[0] - highest)
    late_factor = jnp.exp(later[0] - highest)
    return (
        highest,
        earlier[1] * early_factor + later[1] * late_factor,
        earlier[2] * early_factor + later[2] * late_factor,
        earlier[3] + later[3],
    )


def on_device(hidden, head, chosen):
    row_count = hidden.shape[0]
    columns = head.shape[1]
    levels = chosen.shape[0]
    shard_index = lax.axis_index("codes")
    logits = jnp.dot(hidden, collect(head, "frames", 0), preferred_element_type=jnp.float32)
    group_count = max(columns // CODES, 1)
    level_span = min(columns, CODES)
    first_column = shard_index * columns
    first_level = first_column // CODES
    offset_code = first_column % CODES
    blocks = logits.reshape(row_count, group_count, level_span)
    local_max = jnp.max(blocks, axis=2)
    wanted = lax.dynamic_slice_in_dim(chosen, first_level, group_count, 0).T - offset_code
    matches = wanted[:, :, None] == lax.broadcasted_iota(jnp.int32, (1, 1, level_span), 2)
    picked = jnp.sum(jnp.where(matches, blocks, 0.0), axis=2)
    shifted = jnp.exp(blocks - local_max[:, :, None])
    local_total = jnp.sum(shifted, axis=2)
    local_logit = jnp.sum(shifted * blocks, axis=2)
    sharers = max(CODES // columns, 1)
    current = (local_max[:, 0], local_total[:, 0], local_logit[:, 0], picked[:, 0])
    step_count = sharers.bit_length() - 1
    for step in range(step_count):
        bit_number = step_count - 1 - step
        my_bit = shard_index // 2**bit_number % 2
        halves = tuple((piece.reshape(2, piece.shape[0] // 2) for piece in current))
        keeping = tuple((jnp.where(my_bit == 0, part[0], part[1]) for part in halves))
        sending = tuple((jnp.where(my_bit == 0, part[1], part[0]) for part in halves))
        arrived = partner(sending, "codes", bit_number)
        current = combine(keeping, arrived)
    confidence, entropy = finish(
        current[0][None], current[1][None], current[2][None], current[3][None]
    )
    gathered = gather_together((confidence, entropy), "codes", (0, 0))
    return (gathered[0].reshape(levels, row_count), gathered[1].reshape(levels, row_count))


def solution(mesh):
    placed = (P("frames", None), P("frames", "codes"), P(None, "frames"))
    return jax.shard_map(
        on_device,
        mesh=mesh,
        in_specs=placed,
        out_specs=(P(None, "frames"), P(None, "frames")),
        check_vma=False,
    )
```

profile of v0, /device:TPU:2, one launch (start us, length us, event | category | flops | bytes accessed | tf_op | source)
XLA Modules:
  0.0 91.0 jit_solution(16815592511786878886)
XLA Ops:
  0.6 1.7 %broadcast_in_dim.5 = bf16[8,128,256]{2,1,0:T(8,128)(2,1)} broadcast(bf16[128,256]{1,0:T(8,128)(2,1)} %param.4), dimensions={1,2} | broadcast | bytes 589824 | tf_op jit(solution)/shard_map/broadcast_in_dim | solution.py:11
  2.3 5.6 %all-to-all-start = ((bf16[8,128,256]{2,1,0:T(8,128)(2,1)}), bf16[8,128,256]{2,1,0:T(8,128)(2,1)S(1)}, u32[]{:S(2)}, u32[]{:S(2)}) async-start(bf16[8,128,256]{2,1,0:T(8,128)(2,1)} %broadcast_in_dim.5), calls=%async_computation | async-start | bytes 1048576 | tf_op jit(solution)/shard_map/all_to_all | solution.py:11
  7.9 0.9 %dynamic-slice_subtract_fusion = s32[1,4096]{1,0:T(1,128)S(1)} fusion(s32[8,4096]{1,0:T(8,128)} %param.5, s32[]{:T(128)S(6)} %select_n.109, s32[]{:T(128)S(6)} %select_n.110), kind=kLoop, calls=%fused_computation.5 | loop fusion | flops 4096 | bytes 32776 | tf_op jit(solution)/shard_map/sub | solution.py:75
  8.9 8.0 %all-to-all-done = bf16[8,128,256]{2,1,0:T(8,128)(2,1)S(1)} async-done(((bf16[8,128,256]{2,1,0:T(8,128)(2,1)}), bf16[8,128,256]{2,1,0:T(8,128)(2,1)S(1)}, u32[]{:S(2)}, u32[]{:S(2)}) %all-to-all-start) | async-done | bytes 524320 | tf_op jit(solution)/shard_map/all_to_all | solution.py:11
  16.8 5.8 %fusion.4 = (f32[4096]{0:T(1024)S(1)}, f32[4096,256]{0,1:T(8,128)S(1)}) fusion(bf16[4096,1024]{1,0:T(8,128)(2,1)} %param.3, bf16[1024,256]{1,0:T(8,128)(2,1)S(1)} %bitcast.4), kind=kOutput, calls=%fused_computation.30 | convolution fusion | flops 2148528128 | bytes 13123584 | tf_op jit(solution)/shard_map/dot_general | solution.py:67
  22.6 1.5 %fusion = (f32[4096]{0:T(1024)S(1)}, f32[4096]{0:T(1024)S(1)}, f32[4096]{0:T(1024)S(1)}) fusion(f32[4096,256]{0,1:T(8,128)S(1)} %get-tuple-element.12, f32[4096]{0:T(1024)S(1)} %get-tuple-element.11, s32[4096]{0:T(1024)S(1)} %bitcast.5), kind=kLoop, calls=%fused_computation.2 | loop fusion | flops 7327744 | bytes 4276224 | tf_op jit(solution)/shard_map/reduce_sum | solution.py:79
  24.1 2.5 %collective-permute-start = (f32[2048]{0:T(1024)S(1)}, f32[2048]{0:T(1024)S(1)}, u32[]{:S(2)}, u32[]{:S(2)}) collective-permute-start(f32[2048]{0:T(1024)S(1)} %slice_select_fusion.4), channel_id=1, source_target_pairs={{0,2},{2,0},{1,3},{3,1},{4,6},{6,4},{5,7},{7,5},{8,10},{10,8},{9,1... | collective-permute-start | bytes 24584 | tf_op jit(solution)/shard_map/ppermute | solution.py:32
  26.6 0.5 collective-permute-start.4
  27.1 2.4 %collective-permute-start.2 = (f32[2048]{0:T(1024)S(1)}, f32[2048]{0:T(1024)S(1)}, u32[]{:S(2)}, u32[]{:S(2)}) collective-permute-start(f32[2048]{0:T(1024)S(1)} %slice_select_fusion.2), channel_id=1, source_target_pairs={{0,2},{2,0},{1,3},{3,1},{4,6},{6,4},{5,7},{7,5},{8,10},{10,8},{9,1... | collective-permute-start | bytes 24584 | tf_op jit(solution)/shard_map/ppermute | solution.py:32
  29.6 0.5 collective-permute-start.6
  30.1 0.0 collective-permute-done
  30.1 1.6 %collective-permute-start.1 = (f32[1024]{0:T(1024)S(1)}, f32[1024]{0:T(1024)S(1)}, u32[]{:S(2)}, u32[]{:S(2)}) collective-permute-start(f32[1024]{0:T(1024)S(1)} %slice_select_fusion.9), channel_id=1, source_target_pairs={{0,1},{1,0},{2,3},{3,2},{4,5},{5,4},{6,7},{7,6},{8,9},{9,8},{10,11... | collective-permute-start | bytes 12296 | tf_op jit(solution)/shard_map/ppermute | solution.py:32
  31.7 0.0 collective-permute-done.4
  31.7 0.0 collective-permute-done.2
  31.7 1.6 %collective-permute-start.5 = (f32[1024]{0:T(1024)S(1)}, f32[1024]{0:T(1024)S(1)}, u32[]{:S(2)}, u32[]{:S(2)}) collective-permute-start(f32[1024]{0:T(1024)S(1)} %slice_select_fusion.6), channel_id=1, source_target_pairs={{0,1},{1,0},{2,3},{3,2},{4,5},{5,4},{6,7},{7,6},{8,9},{9,8},{10,11... | collective-permute-start | bytes 12296 | tf_op jit(solution)/shard_map/ppermute | solution.py:32
  33.3 0.5 collective-permute-start.3
  33.8 0.3 collective-permute-done.6
  34.1 2.0 %collective-permute-start.7 = (f32[1024]{0:T(1024)S(1)}, f32[1024]{0:T(1024)S(1)}, u32[]{:S(2)}, u32[]{:S(2)}) collective-permute-start(f32[1024]{0:T(1024)S(1)} %slice_select_fusion.5), channel_id=1, source_target_pairs={{0,1},{1,0},{2,3},{3,2},{4,5},{5,4},{6,7},{7,6},{8,9},{9,8},{10,11... | collective-permute-start | bytes 12296 | tf_op jit(solution)/shard_map/ppermute | solution.py:32
  36.1 0.0 collective-permute-done.1
  36.2 0.8 collective-permute-done.3
  36.9 0.9 collective-permute-done.7
  37.9 51.6 %all-gather = f32[65536]{0:T(1024)S(1)} all-gather(f32[2048]{0:T(1024)S(1)} %pad_maximum_fusion), channel_id=2, replica_groups=mesh['frames'=8,'codes'=32] {'codes'}, dimensions={0}, use_global_device_ids=true | all-gather | bytes 270336 | tf_op jit(solution)/shard_map/all_gather | solution.py:37
  89.5 0.7 reshape_reshape_reshape.6
  90.2 0.7 reshape_reshape_reshape.7
  (16 shorter events, 0.2 us)
Async XLA Ops:
  2.3 14.5 %all-to-all-start = ((bf16[8,128,256]{2,1,0:T(8,128)(2,1)}), bf16[8,128,256]{2,1,0:T(8,128)(2,1)S(1)}, u32[]{:S(2)}, u32[]{:S(2)}) async-start(bf16[8,128,256]{2,1,0:T(8,128)(2,1)} %broadcast_in_dim.5), calls=%async_computation | async-start | bytes 1048576 | tf_op jit(solution)/shard_map/all_to_all | solution.py:11
  24.1 6.0 %collective-permute-start = (f32[2048]{0:T(1024)S(1)}, f32[2048]{0:T(1024)S(1)}, u32[]{:S(2)}, u32[]{:S(2)}) collective-permute-start(f32[2048]{0:T(1024)S(1)} %slice_select_fusion.4), channel_id=1, source_target_pairs={{0,2},{2,0},{1,3},{3,1},{4,6},{6,4},{5,7},{7,5},{8,10},{10,8},{9,1... | collective-permute-start | bytes 24584 | tf_op jit(solution)/shard_map/ppermute | solution.py:32
  26.6 5.1 %collective-permute-start.4 = (f32[2048]{0:T(1024)S(1)}, f32[2048]{0:T(1024)S(1)}, u32[]{:S(2)}, u32[]{:S(2)}) collective-permute-start(f32[2048]{0:T(1024)S(1)} %slice_select_fusion.1), channel_id=1, source_target_pairs={{0,2},{2,0},{1,3},{3,1},{4,6},{6,4},{5,7},{7,5},{8,10},{10,8},{9,1... | collective-permute-start | bytes 24584 | tf_op jit(solution)/shard_map/ppermute | solution.py:32
  27.1 4.6 %collective-permute-start.2 = (f32[2048]{0:T(1024)S(1)}, f32[2048]{0:T(1024)S(1)}, u32[]{:S(2)}, u32[]{:S(2)}) collective-permute-start(f32[2048]{0:T(1024)S(1)} %slice_select_fusion.2), channel_id=1, source_target_pairs={{0,2},{2,0},{1,3},{3,1},{4,6},{6,4},{5,7},{7,5},{8,10},{10,8},{9,1... | collective-permute-start | bytes 24584 | tf_op jit(solution)/shard_map/ppermute | solution.py:32
  29.6 4.5 %collective-permute-start.6 = (f32[2048]{0:T(1024)S(1)}, f32[2048]{0:T(1024)S(1)}, u32[]{:S(2)}, u32[]{:S(2)}) collective-permute-start(f32[2048]{0:T(1024)S(1)} %slice_select_fusion), channel_id=1, source_target_pairs={{0,2},{2,0},{1,3},{3,1},{4,6},{6,4},{5,7},{7,5},{8,10},{10,8},{9,1... | collective-permute-start | bytes 24584 | tf_op jit(solution)/shard_map/ppermute | solution.py:32
  30.1 6.1 %collective-permute-start.1 = (f32[1024]{0:T(1024)S(1)}, f32[1024]{0:T(1024)S(1)}, u32[]{:S(2)}, u32[]{:S(2)}) collective-permute-start(f32[1024]{0:T(1024)S(1)} %slice_select_fusion.9), channel_id=1, source_target_pairs={{0,1},{1,0},{2,3},{3,2},{4,5},{5,4},{6,7},{7,6},{8,9},{9,8},{10,11... | collective-permute-start | bytes 12296 | tf_op jit(solution)/shard_map/ppermute | solution.py:32
  31.7 4.4 %collective-permute-start.5 = (f32[1024]{0:T(1024)S(1)}, f32[1024]{0:T(1024)S(1)}, u32[]{:S(2)}, u32[]{:S(2)}) collective-permute-start(f32[1024]{0:T(1024)S(1)} %slice_select_fusion.6), channel_id=1, source_target_pairs={{0,1},{1,0},{2,3},{3,2},{4,5},{5,4},{6,7},{7,6},{8,9},{9,8},{10,11... | collective-permute-start | bytes 12296 | tf_op jit(solution)/shard_map/ppermute | solution.py:32
  33.3 3.6 %collective-permute-start.3 = (f32[1024]{0:T(1024)S(1)}, f32[1024]{0:T(1024)S(1)}, u32[]{:S(2)}, u32[]{:S(2)}) collective-permute-start(f32[1024]{0:T(1024)S(1)} %slice_select_fusion.7), channel_id=1, source_target_pairs={{0,1},{1,0},{2,3},{3,2},{4,5},{5,4},{6,7},{7,6},{8,9},{9,8},{10,11... | collective-permute-start | bytes 12296 | tf_op jit(solution)/shard_map/ppermute | solution.py:32
  34.1 3.7 %collective-permute-start.7 = (f32[1024]{0:T(1024)S(1)}, f32[1024]{0:T(1024)S(1)}, u32[]{:S(2)}, u32[]{:S(2)}) collective-permute-start(f32[1024]{0:T(1024)S(1)} %slice_select_fusion.5), channel_id=1, source_target_pairs={{0,1},{1,0},{2,3},{3,2},{4,5},{5,4},{6,7},{7,6},{8,9},{9,8},{10,11... | collective-permute-start | bytes 12296 | tf_op jit(solution)/shard_map/ppermute | solution.py:32
where the time goes:
time: 91.6 us; the launch traced here: 91 us
  blocking collectives  51.6 us (56%)
  starting transfers between devices  17.3 us (19%)
  waiting for transfers between devices  9.93 us (11%)
  matrix products  5.79 us (6%)
  local copies, waits for them, and re-layouts  3.16 us (3%)
  other arithmetic  2.47 us (3%)
    all_gather x1, blocking collectives, gather_together(): lines, at, outs = (lax.all_gather(line, axis), 0, [])  51.6 us
    ppermute x8, starting transfers between devices, partner(): return lax.ppermute(block, axis, route)  11.7 us
    all_to_all x1, waiting for transfers between devices, from_everyone(): lax.all_to_all(jnp.broadcast_to(x[None], (count, *x.shape)), axis, 0, 0,...  7.97 us
    dot_general x1, matrix products, on_device(): jnp.dot(hidden, collect(head, 'frames', 0), preferred_element_type=jnp.fl...  5.79 us
    all_to_all x1, starting transfers between devices, from_everyone(): lax.all_to_all(jnp.broadcast_to(x[None], (count, *x.shape)), axis, 0, 0,...  5.64 us
    ppermute x8, waiting for transfers between devices, partner(): return lax.ppermute(block, axis, route)  1.97 us
  transfers between devices with their start and end apart: 9, of which 4 were waited for; matrix products, arithmetic and copies ran while one was open for 1% of the time, Pallas kernels for 0%

commit v1 on v0

v1 whole, which is shorter than its diff:
```python
import functools
import math

import jax
import jax.numpy as jnp
from jax import lax
from jax.experimental import pallas as pl
from jax.experimental.pallas import tpu as pltpu
from jax.sharding import PartitionSpec as P

CODES = 1024
LOG2E = math.log2(math.e)
LN2 = math.log(2.0)
MESH = pl.DeviceIdType.MESH
LANES = 128
TILE = 256


def tile_stats(scaled, wanted):
    flipped = scaled.T
    columns, frames = flipped.shape
    top = jnp.max(flipped, axis=0, keepdims=True)
    below = flipped - top
    powers = jnp.exp2(below)
    total = jnp.sum(powers, axis=0, keepdims=True)
    weighted = jnp.sum(powers * below, axis=0, keepdims=True)
    groups = columns // 8
    pool = flipped.reshape(groups, 8, frames)
    spread = jnp.broadcast_to(wanted, (8, frames))
    bit = groups.bit_length() - 2
    while bit >= 0:
        half = 1 << bit
        upper = (lax.shift_right_arithmetic(spread, 3 + bit) & 1) == 1
        pool = jnp.where(upper[None], pool[half:], pool[:half])
        bit -= 1
    row = lax.broadcasted_iota(jnp.int32, (8, frames), 0)
    here = (row == (spread & 7)) & (spread >= 0) & (spread < columns)
    picked = jnp.sum(jnp.where(here, pool[0], 0.0), axis=0, keepdims=True)
    return top, total, weighted, picked


def kernel(
    xs, ys, zs,
    hidden_hbm, head_hbm, chosen_ref, conf_ref, ent_ref,
    hid, weights, acc, outgoing, incoming, final,
    load_sem, wsend, wrecv, ssend, srecv, gsend, gzrecv, gyrecv,
):
    fidx = lax.axis_index("frames")
    cidx = lax.axis_index("codes")
    x, core = fidx // 2, fidx % 2
    y, z = cidx // zs, cidx % zs
    q, quad = z % 4, z // 4
    level = y * (zs // 4) + quad
    sib = 1 - core
    xl, xr, xo = (x + xs - 1) % xs, (x + 1) % xs, (x + 2) % xs

    def at(px, pcore, py, pz):
        return (px * 2 + pcore, py * zs + pz)

    own_head = pltpu.make_async_copy(head_hbm, weights.at[fidx], load_sem.at[0])
    own_head.start()
    quarter = hid.shape[0] // 4
    loads = []
    for i in range(4):
        rows = pl.ds(i * quarter, quarter)
        copy = pltpu.make_async_copy(hidden_hbm.at[rows], hid.at[rows], load_sem.at[1 + i])
        copy.start()
        loads.append(copy)

    z_peers = [(z + d) % zs for d in (1, zs - 1, 2, zs - 2, 3, zs - 3, 4)]
    y_peers = [(y + d) % ys for d in (1, ys - 1, 2)]
    barrier = pltpu.get_barrier_semaphore()
    peers = [at(x, sib, y, z), at(xl, core, y, z), at(xr, core, y, z)]
    peers += [at(x, core, y, pz) for pz in z_peers]
    peers += [at(x, core, py, z) for py in y_peers]
    for peer in peers:
        pl.semaphore_signal(barrier, inc=1, device_id=peer, device_id_type=MESH)
    pl.semaphore_wait(barrier, len(peers))
    own_head.wait()

    half = weights.shape[1] // 2

    def piece(slot, part):
        if part is None:
            return weights.at[slot]
        return weights.at[slot, pl.ds(part * half, half)]

    sends = []

    def push(slot, part, index, peer):
        copy = pltpu.make_async_remote_copy(
            src_ref=piece(slot, part), dst_ref=piece(slot, part),
            send_sem=wsend.at[index], recv_sem=wrecv.at[index],
            device_id=peer, device_id_type=MESH,
        )
        copy.start()
        sends.append(copy)

    def landed(slot, part, index):
        pltpu.make_async_remote_copy(
            src_ref=piece(slot, part), dst_ref=piece(slot, part),
            send_sem=wsend.at[index], recv_sem=wrecv.at[index],
            device_id=at(x, sib, y, z), device_id_type=MESH,
        ).wait_recv()

    mate = at(x, sib, y, z)
    left, right = at(xl, core, y, z), at(xr, core, y, z)
    push(fidx, 0, 1, right)
    push(fidx, 1, 4, left)
    push(fidx, None, 0, mate)
    push(fidx, 1, 2, right)
    push(fidx, 0, 3, left)
    left_slot, right_slot, far_slot = xl * 2 + core, xr * 2 + core, xo * 2 + core
    landed(left_slot, 0, 1)
    push(left_slot, 0, 5, right)
    landed(right_slot, 1, 4)
    push(right_slot, 1, 6, left)
    landed(left_slot, 1, 2)
    push(left_slot, None, 7, mate)
    landed(right_slot, 0, 3)
    push(right_slot, None, 8, mate)

    depth = 2 * weights.shape[1]

    def product(rows, chip):
        pair = weights[pl.ds(chip * 2, 2)].reshape(depth, weights.shape[2])
        cols = pl.ds(pl.multiple_of(chip * depth, depth), depth)
        return jnp.dot(hid[rows, cols], pair, preferred_element_type=jnp.float32)

    landed(x * 2 + sib, None, 0)
    step = 512
    for i in range(4):
        loads[i].wait()
    for i in range(hid.shape[0] // step):
        rows = pl.ds(i * step, step)
        acc[rows] = product(rows, x)
    landed(far_slot, 0, 5)
    push(far_slot, 0, 9, mate)
    landed(far_slot, 1, 6)
    push(far_slot, 1, 10, mate)
    landed(xl * 2 + sib, None, 7)
    landed(xr * 2 + sib, None, 8)
    for i in range(hid.shape[0] // step):
        rows = pl.ds(i * step, step)
        acc[rows] += product(rows, xl) + product(rows, xr)
    landed(xo * 2 + sib, 0, 9)
    landed(xo * 2 + sib, 1, 10)

    offset = q * weights.shape[2]
    low = q < 2
    order = [jnp.where(low, 3, 0), jnp.where(low, 2, 1)]
    order.append(jnp.where(low, jnp.where(q == 1, 0, 1), jnp.where(q == 2, 3, 2)))
    order.append(q)
    stat_sends = []
    for s in range(4):
        part = order[s]
        for t in range(quarter // TILE):
            rows = pl.ds(pl.multiple_of(part * quarter + t * TILE, TILE), TILE)
            scaled = (acc[rows] + product(rows, xo)) * LOG2E
            wanted = chosen_ref[pl.ds(level, 1), rows] - offset
            stats = tile_stats(scaled, wanted)
            for k in range(4):
                for i in range(TILE // LANES):
                    outgoing[part, k, pl.ds(t * (TILE // LANES) + i, 1), :] = stats[k][:, i * LANES:(i + 1) * LANES]
        if s < 3:
            copy = pltpu.make_async_remote_copy(
                src_ref=outgoing.at[part], dst_ref=incoming.at[q],
                send_sem=ssend.at[s], recv_sem=srecv.at[q],
                device_id=at(x, core, y, quad * 4 + part), device_id_type=MESH,
            )
            copy.start()
            stat_sends.append(copy)

    found = [tuple(outgoing[q, k] for k in range(4))]
    for s in range(3):
        part = order[s]
        pltpu.make_async_remote_copy(
            src_ref=outgoing.at[part], dst_ref=incoming.at[part],
            send_sem=ssend.at[s], recv_sem=srecv.at[part],
            device_id=at(x, core, y, quad * 4 + part), device_id_type=MESH,
        ).wait_recv()
        found.append(tuple(incoming[part, k] for k in range(4)))
    top = functools.reduce(jnp.maximum, [f[0] for f in found])
    total = weighted = picked = jnp.zeros_like(top)
    for own_top, own_total, own_weighted, own_picked in found:
        gap = own_top - top
        factor = jnp.exp2(gap)
        total += factor * own_total
        weighted += factor * (own_weighted + gap * own_total)
        picked += own_picked
    bits = jnp.log(total)
    final[cidx, 0] = (picked - top) * LN2 - bits
    final[cidx, 1] = bits - LN2 * (weighted / total)

    z_offsets = (1, zs - 1, 2, zs - 2, 3, zs - 3, 4)
    last = []

    def spread(block, index, recv, peer):
        copy = pltpu.make_async_remote_copy(
            src_ref=final.at[block], dst_ref=final.at[block],
            send_sem=gsend.at[index], recv_sem=recv,
            device_id=peer, device_id_type=MESH,
        )
        copy.start()
        last.append(copy)

    def arrived(block, recv):
        pltpu.make_async_remote_copy(
            src_ref=final.at[block], dst_ref=final.at[block],
            send_sem=gsend.at[0], recv_sem=recv,
            device_id=mate, device_id_type=MESH,
        ).wait_recv()

    for n, d in enumerate(reversed(z_offsets)):
        spread(cidx, n, gzrecv.at[d], at(x, core, y, (z + d) % zs))
    y_offsets = (2, 1, ys - 1)
    count = len(z_offsets)

    def onward(pz, d_index):
        nonlocal count
        for d in y_offsets:
            spread(y * zs + pz, count, gyrecv.at[d, d_index], at(x, core, (y + d) % ys, z))
            count += 1

    onward(z, 0)
    for d in z_offsets:
        pz = (z + zs - d) % zs
        arrived(y * zs + pz, gzrecv.at[d])
        onward(pz, d)
    for d in (1, ys - 1, 2):
        py = (y + ys - d) % ys
        for dz in (0,) + z_offsets:
            arrived(py * zs + (z + zs - dz) % zs, gyrecv.at[d, dz])

    blocks = final.shape[0]
    levels = conf_ref.shape[0]
    for part in range(4):
        for j in range(8):
            cols = pl.ds(part * quarter + j * LANES, LANES)
            for k, out in ((0, conf_ref), (1, ent_ref)):
                out[:, cols] = jnp.concatenate(
                    [final[g * 4 + part, k, pl.ds(j, 1), :] for g in range(levels)], axis=0
                )
    for copy in sends + stat_sends + last:
        copy.wait_send()


def on_device(xs, ys, zs, hidden, head, chosen):
    rows, width = hidden.shape
    depth, columns = head.shape
    levels = chosen.shape[0]
    quarter = rows // 4
    dma = pltpu.SemaphoreType.DMA
    out = jax.ShapeDtypeStruct((levels, rows), jnp.float32)
    vmem = pl.BlockSpec(memory_space=pltpu.VMEM)
    anywhere = pl.BlockSpec(memory_space=pl.ANY)
    return pl.pallas_call(
        functools.partial(kernel, xs, ys, zs),
        out_shape=(out, out),
        in_specs=[anywhere, anywhere, vmem],
        out_specs=(vmem, vmem),
        scratch_shapes=[
            pltpu.VMEM((rows, width), jnp.bfloat16),
            pltpu.VMEM((width // depth, depth, columns), jnp.bfloat16),
            pltpu.VMEM((rows, columns), jnp.float32),
            pltpu.VMEM((4, 4, quarter // LANES, LANES), jnp.float32),
            pltpu.VMEM((4, 4, quarter // LANES, LANES), jnp.float32),
            pltpu.VMEM((ys * zs, 2, quarter // LANES, LANES), jnp.float32),
            dma((5,)), dma((11,)), dma((11,)), dma((3,)), dma((4,)), dma((31,)), dma((8,)), dma((4, 8)),
        ],
        compiler_params=pltpu.CompilerParams(collective_id=0, has_side_effects=True),
    )(hidden, head, chosen)


def solution(mesh):
    return jax.shard_map(
        functools.partial(on_device, mesh.shape["frames"] // 2, 4, mesh.shape["codes"] // 4),
        mesh=mesh,
        in_specs=(P("frames", None), P("frames", "codes"), P(None, "frames")),
        out_specs=(P(None, "frames"), P(None, "frames")),
        check_vma=False,
    )
```

time: 91.6 us -> 35.7 us (0.39)
  blocking collectives: 51.6 us -> 0 us
  Pallas kernels: 0 us -> 31.8 us
  starting transfers between devices: 17.3 us -> 0 us
  waiting for transfers between devices: 9.93 us -> 0 us
  matrix products: 5.79 us -> 0 us
  other arithmetic: 2.47 us -> 0 us
    all_gather x1 -> x0, blocking collectives: 51.6 us -> none  [gather_together(): lines, at, outs = (lax.all_gather(line, axis), 0, [])]
    pallas_call x0 -> x1, Pallas kernels: none -> 31.8 us  [on_device(): pl.pallas_call(functools.partial(kernel, xs, ys, zs), out_shape=(out, out...]
    ppermute x8 -> x0, starting transfers between devices: 11.7 us -> none  [partner(): return lax.ppermute(block, axis, route)]
    all_to_all x1 -> x0, waiting for transfers between devices: 7.97 us -> none  [from_everyone(): lax.all_to_all(jnp.broadcast_to(x[None], (count, *x.shape)), axis, 0, 0,...]
    dot_general x1 -> x0, matrix products: 5.79 us -> none  [on_device(): jnp.dot(hidden, collect(head, 'frames', 0), preferred_element_type=jnp.fl...]
    all_to_all x1 -> x0, starting transfers between devices: 5.64 us -> none  [from_everyone(): lax.all_to_all(jnp.broadcast_to(x[None], (count, *x.shape)), axis, 0, 0,...]
    unnamed x0 -> x2, local copies, waits for them, and re-layouts: none -> 3.14 us
    ppermute x8 -> x0, waiting for transfers between devices: 1.97 us -> none  [partner(): return lax.ppermute(block, axis, route)]
  transfers between devices with their start and end apart: 9 -> 0, of which waited for: 4 -> 0; matrix products, arithmetic and copies ran while one was open for 1% -> 0% of each run, Pallas kernels for 0% -> 0%
where the time goes in v1:
time: 35.7 us; the launch traced here: 35.6 us
  Pallas kernels  31.8 us (89%)
  local copies, waits for them, and re-layouts  3.14 us (9%)
  between operations  0.64 us (2%)
    pallas_call x1, Pallas kernels, on_device(): pl.pallas_call(functools.partial(kernel, xs, ys, zs), out_shape=(out, out...  31.8 us
    unnamed x2, local copies, waits for them, and re-layouts  3.14 us

profile of v1, /device:TPU:2, one launch (start us, length us, event | category | flops | bytes accessed | tf_op | source)
XLA Modules:
  0.0 35.6 jit_solution(2539277770136095311)
XLA Ops:
  0.6 31.8 %shard_map.50 = (f32[8,4096]{1,0:T(8,128)}, f32[8,4096]{1,0:T(8,128)}) custom-call(bf16[4096,1024]{1,0:T(8,128)(2,1)} %hidden_hbm.1, bf16[128,256]{1,0:T(8,128)(2,1)} %head_hbm.1, s32[8,4096]{1,0:T(8,128)} %chosen_ref.1), custom_call_target="tpu_custom_call" | custom-call | tf_op jit(solution)/shard_map/pallas_call | solution.py:257
  32.5 1.6 %copy.7 = f32[8,4096]{1,0:T(8,128)} copy(f32[8,4096]{1,0:T(8,128)} %get-tuple-element.4) | data formatting | bytes 262144
  34.0 1.6 %copy.8 = f32[8,4096]{1,0:T(8,128)} copy(f32[8,4096]{1,0:T(8,128)} %get-tuple-element.5) | data formatting | bytes 262144

commit v2 on v1

--- a/solution.py
+++ b/solution.py
@@ -14,6 +14,19 @@
 MESH = pl.DeviceIdType.MESH
 LANES = 128
 TILE = 256
+PROFILE = False
+
+
+open_scopes = []
+
+
+def mark(name):
+    if PROFILE:
+        while open_scopes:
+            open_scopes.pop().__exit__(None, None, None)
+        if name:
+            open_scopes.append(jax.named_scope(name))
+            open_scopes[-1].__enter__()
 
 
 def tile_stats(scaled, wanted):
@@ -41,9 +54,9 @@
 
 def kernel(
     xs, ys, zs,
-    hidden_hbm, head_hbm, chosen_ref, conf_ref, ent_ref,
-    hid, weights, acc, outgoing, incoming, final,
-    load_sem, wsend, wrecv, ssend, srecv, gsend, gzrecv, gyrecv,
+    hidden_hbm, head_hbm, chosen_hbm, final,
+    hid, weights, acc, outgoing, incoming, chosen_ref,
+    load_sem, wsend, wrecv, ssend, srecv, gsend, gzrecv, gyrecv, near_sem, wide_sem, side_sem,
 ):
     fidx = lax.axis_index("frames")
     cidx = lax.axis_index("codes")
@@ -57,8 +70,10 @@
     def at(px, pcore, py, pz):
         return (px * 2 + pcore, py * zs + pz)
 
+    mark("p00issue")
     own_head = pltpu.make_async_copy(head_hbm, weights.at[fidx], load_sem.at[0])
     own_head.start()
+    chosen_load = pltpu.make_async_copy(chosen_hbm, chosen_ref, load_sem.at[5])
     quarter = hid.shape[0] // 4
     loads = []
     for i in range(4):
@@ -67,17 +82,25 @@
         copy.start()
         loads.append(copy)
 
-    z_peers = [(z + d) % zs for d in (1, zs - 1, 2, zs - 2, 3, zs - 3, 4)]
-    y_peers = [(y + d) % ys for d in (1, ys - 1, 2)]
+    mark("p01barrier")
+    mate = at(x, sib, y, z)
+    left, right = at(xl, core, y, z), at(xr, core, y, z)
+    z_near = [at(x, core, y, (z + d) % zs) for d in (1, zs - 1)]
+    z_wide = [at(x, core, y, (z + d) % zs) for d in (2, zs - 2)]
+    y_near = [at(x, core, (y + d) % ys, z) for d in (1, ys - 1)]
     barrier = pltpu.get_barrier_semaphore()
-    peers = [at(x, sib, y, z), at(xl, core, y, z), at(xr, core, y, z)]
-    peers += [at(x, core, y, pz) for pz in z_peers]
-    peers += [at(x, core, py, z) for py in y_peers]
-    for peer in peers:
+    around = [mate, left, right, at(xo, core, y, z)] + z_near + y_near
+    for peer in around:
         pl.semaphore_signal(barrier, inc=1, device_id=peer, device_id_type=MESH)
-    pl.semaphore_wait(barrier, len(peers))
+    chosen_load.start()
+    pl.semaphore_wait(barrier, len(around))
+    for peer in z_near:
+        pl.semaphore_signal(near_sem, inc=1, device_id=peer, device_id_type=MESH)
+    for peer in y_near:
+        pl.semaphore_signal(side_sem, inc=1, device_id=peer, device_id_type=MESH)
     own_head.wait()
 
+    mark("p02gather")
     half = weights.shape[1] // 2
 
     def piece(slot, part):
@@ -103,23 +126,20 @@
             device_id=at(x, sib, y, z), device_id_type=MESH,
         ).wait_recv()
 
-    mate = at(x, sib, y, z)
-    left, right = at(xl, core, y, z), at(xr, core, y, z)
-    push(fidx, 0, 1, right)
-    push(fidx, 1, 4, left)
     push(fidx, None, 0, mate)
-    push(fidx, 1, 2, right)
-    push(fidx, 0, 3, left)
+    push(fidx, None, 1, right)
+    push(fidx, None, 2, left)
+    push(fidx, None, 3, at(xo, core, y, z))
+    pl.semaphore_wait(near_sem, 2)
+    for peer in z_wide:
+        pl.semaphore_signal(wide_sem, inc=1, device_id=peer, device_id_type=MESH)
     left_slot, right_slot, far_slot = xl * 2 + core, xr * 2 + core, xo * 2 + core
-    landed(left_slot, 0, 1)
-    push(left_slot, 0, 5, right)
-    landed(right_slot, 1, 4)
-    push(right_slot, 1, 6, left)
-    landed(left_slot, 1, 2)
-    push(left_slot, None, 7, mate)
-    landed(right_slot, 0, 3)
-    push(right_slot, None, 8, mate)
-
+    landed(left_slot, None, 1)
+    push(left_slot, None, 4, mate)
+    landed(right_slot, None, 2)
+    push(right_slot, None, 5, mate)
+
+    mark("p03ownmm")
     depth = 2 * weights.shape[1]
 
     def product(rows, chip):
@@ -134,18 +154,22 @@
     for i in range(hid.shape[0] // step):
         rows = pl.ds(i * step, step)
         acc[rows] = product(rows, x)
-    landed(far_slot, 0, 5)
-    push(far_slot, 0, 9, mate)
-    landed(far_slot, 1, 6)
-    push(far_slot, 1, 10, mate)
-    landed(xl * 2 + sib, None, 7)
-    landed(xr * 2 + sib, None, 8)
+    mark("p04far")
+    landed(far_slot, None, 3)
+    push(far_slot, None, 6, mate)
+    mark("p05sidemm")
+    landed(xl * 2 + sib, None, 4)
+    landed(xr * 2 + sib, None, 5)
     for i in range(hid.shape[0] // step):
         rows = pl.ds(i * step, step)
         acc[rows] += product(rows, xl) + product(rows, xr)
-    landed(xo * 2 + sib, 0, 9)
-    landed(xo * 2 + sib, 1, 10)
-
+    mark("p06farwait")
+    landed(xo * 2 + sib, None, 6)
+
+    mark("p07stats")
+    pl.semaphore_wait(wide_sem, 2)
+    pl.semaphore_wait(side_sem, 2)
+    chosen_load.wait()
     offset = q * weights.shape[2]
     low = q < 2
     order = [jnp.where(low, 3, 0), jnp.where(low, 2, 1)]
@@ -171,6 +195,7 @@
             copy.start()
             stat_sends.append(copy)
 
+    mark("p08statwait")
     found = [tuple(outgoing[q, k] for k in range(4))]
     for s in range(3):
         part = order[s]
@@ -192,6 +217,7 @@
     final[cidx, 0] = (picked - top) * LN2 - bits
     final[cidx, 1] = bits - LN2 * (weighted / total)
 
+    mark("p09spread")
     z_offsets = (1, zs - 1, 2, zs - 2, 3, zs - 3, 4)
     last = []
 
@@ -227,22 +253,33 @@
         pz = (z + zs - d) % zs
         arrived(y * zs + pz, gzrecv.at[d])
         onward(pz, d)
+    mark("p10ywait")
     for d in (1, ys - 1, 2):
         py = (y + ys - d) % ys
         for dz in (0,) + z_offsets:
             arrived(py * zs + (z + zs - dz) % zs, gyrecv.at[d, dz])
 
-    blocks = final.shape[0]
-    levels = conf_ref.shape[0]
-    for part in range(4):
-        for j in range(8):
-            cols = pl.ds(part * quarter + j * LANES, LANES)
-            for k, out in ((0, conf_ref), (1, ent_ref)):
+    mark("p11drain")
+    for copy in sends + stat_sends + last:
+        copy.wait_send()
+    mark(None)
+
+
+def lay_out(final, conf_hbm, ent_hbm, conf, ent, sems):
+    levels, rows = conf.shape
+    copies = []
+    for k, (out, dst) in enumerate(((conf, conf_hbm), (ent, ent_hbm))):
+        for part in range(4):
+            for j in range(rows // 4 // LANES):
+                cols = pl.ds(part * (rows // 4) + j * LANES, LANES)
                 out[:, cols] = jnp.concatenate(
                     [final[g * 4 + part, k, pl.ds(j, 1), :] for g in range(levels)], axis=0
                 )
-    for copy in sends + stat_sends + last:
-        copy.wait_send()
+        copy = pltpu.make_async_copy(out, dst, sems.at[k])
+        copy.start()
+        copies.append(copy)
+    for copy in copies:
+        copy.wait()
 
 
 def on_device(xs, ys, zs, hidden, head, chosen):
@@ -253,23 +290,32 @@
     dma = pltpu.SemaphoreType.DMA
     out = jax.ShapeDtypeStruct((levels, rows), jnp.float32)
     vmem = pl.BlockSpec(memory_space=pltpu.VMEM)
-    anywhere = pl.BlockSpec(memory_space=pl.ANY)
-    return pl.pallas_call(
+    anywhere = pl.BlockSpec(memory_space=pltpu.HBM)
+    final = pl.pallas_call(
         functools.partial(kernel, xs, ys, zs),
-        out_shape=(out, out),
-        in_specs=[anywhere, anywhere, vmem],
-        out_specs=(vmem, vmem),
+        out_shape=pltpu.VMEM((ys * zs, 2, quarter // LANES, LANES), jnp.float32),
+        in_specs=[anywhere, anywhere, anywhere],
+        out_specs=vmem,
         scratch_shapes=[
             pltpu.VMEM((rows, width), jnp.bfloat16),
             pltpu.VMEM((width // depth, depth, columns), jnp.bfloat16),
             pltpu.VMEM((rows, columns), jnp.float32),
             pltpu.VMEM((4, 4, quarter // LANES, LANES), jnp.float32),
             pltpu.VMEM((4, 4, quarter // LANES, LANES), jnp.float32),
-            pltpu.VMEM((ys * zs, 2, quarter // LANES, LANES), jnp.float32),
-            dma((5,)), dma((11,)), dma((11,)), dma((3,)), dma((4,)), dma((31,)), dma((8,)), dma((4, 8)),
+            pltpu.VMEM((levels, rows), jnp.int32),
+            dma((6,)), dma((11,)), dma((11,)), dma((3,)), dma((4,)), dma((31,)), dma((8,)), dma((4, 8)),
+            pltpu.SemaphoreType.REGULAR, pltpu.SemaphoreType.REGULAR, pltpu.SemaphoreType.REGULAR,
         ],
-        compiler_params=pltpu.CompilerParams(collective_id=0, has_side_effects=True),
+        compiler_params=pltpu.CompilerParams(collective_id=0, has_side_effects=True, vmem_limit_bytes=56 << 20),
     )(hidden, head, chosen)
+    return pl.pallas_call(
+        lay_out,
+        out_shape=(out, out),
+        in_specs=[vmem],
+        out_specs=(anywhere, anywhere),
+        scratch_shapes=[pltpu.VMEM((levels, rows), jnp.float32)] * 2 + [dma((2,))],
+        compiler_params=pltpu.CompilerParams(vmem_limit_bytes=4 << 20),
+    )(final)
 
 
 def solution(mesh):

time: 35.7 us -> 29.5 us (0.83)
  local copies, waits for them, and re-layouts: 3.14 us -> 0 us
  Pallas kernels: 31.8 us -> 28.7 us
    unnamed x2 -> x0, local copies, waits for them, and re-layouts: 3.14 us -> none
    pallas_call x1 -> x2, Pallas kernels: 31.8 us -> 28.7 us  [the longest x1 27.9 us: on_device(): pl.pallas_call(functools.partial(kernel, xs, ys, zs), out_shape=pltpu.VME...]
where the time goes in v2:
time: 29.5 us; the launch traced here: 29.4 us
  Pallas kernels  28.7 us (97%)
  between operations  0.64 us (2%)
    pallas_call x1, Pallas kernels, on_device(): pl.pallas_call(functools.partial(kernel, xs, ys, zs), out_shape=pltpu.VME...  27.9 us
    pallas_call x1, Pallas kernels, on_device(): pl.pallas_call(lay_out, out_shape=(out, out), in_specs=[vmem], out_specs=...  0.81 us

profile of v2, /device:TPU:2, one launch (start us, length us, event | category | flops | bytes accessed | tf_op | source)
XLA Modules:
  0.0 29.4 jit_solution(14940520633386274137)
XLA Ops:
  0.6 27.9 %shard_map.50.final = f32[32,2,8,128]{3,2,1,0:T(8,128)S(1)} custom-call(bf16[4096,1024]{1,0:T(8,128)(2,1)} %hidden_hbm.1, bf16[128,256]{1,0:T(8,128)(2,1)} %head_hbm.1, s32[8,4096]{1,0:T(8,128)} %chosen_hbm.1), custom_call_target="tpu_custom_call" | custom-call | tf_op jit(solution)/shard_map/pallas_call | solution.py:294
  28.6 0.8 %shard_map.51 = (f32[8,4096]{1,0:T(8,128)}, f32[8,4096]{1,0:T(8,128)}) custom-call(f32[32,2,8,128]{3,2,1,0:T(8,128)S(1)} %shard_map.50.final), custom_call_target="tpu_custom_call" | custom-call | tf_op jit(solution)/shard_map/pallas_call | solution.py:311

commit v3 on v2

v3 whole, which is shorter than its diff:
```python
import functools
import math

import jax
import jax.numpy as jnp
from jax import lax
from jax.experimental import pallas as pl
from jax.experimental.pallas import tpu as pltpu
from jax.sharding import PartitionSpec as P

CODES = 1024
LOG2E = math.log2(math.e)
LN2 = math.log(2.0)
MESH = pl.DeviceIdType.MESH
LANES = 128
TILE = 128
BLOCK = 256
PUSHES = 7
CONF_CODE = (64.0, 20500.0)
ENT_CODE = (1024.0, 6.95)
PROFILE = False


open_scopes = []


def mark(name):
    if PROFILE:
        while open_scopes:
            open_scopes.pop().__exit__(None, None, None)
        if name:
            open_scopes.append(jax.named_scope(name))
            open_scopes[-1].__enter__()


def tile_stats(scaled, wanted):
    flipped = scaled.T
    columns, frames = flipped.shape
    top = jnp.max(flipped, axis=0, keepdims=True)
    below = flipped - top
    powers = jnp.exp2(below)
    total = jnp.sum(powers, axis=0, keepdims=True)
    weighted = jnp.sum(powers * below, axis=0, keepdims=True)
    groups = columns // 8
    pool = flipped.reshape(groups, 8, frames)
    spread = jnp.broadcast_to(wanted, (8, frames))
    bit = groups.bit_length() - 2
    while bit >= 0:
        half = 1 << bit
        upper = (lax.shift_right_arithmetic(spread, 3 + bit) & 1) == 1
        pool = jnp.where(upper[None], pool[half:], pool[:half])
        bit -= 1
    row = lax.broadcasted_iota(jnp.int32, (8, frames), 0)
    here = (row == (spread & 7)) & (spread >= 0) & (spread < columns)
    picked = jnp.sum(jnp.where(here, pool[0], 0.0), axis=0, keepdims=True)
    return top, total, weighted, picked


def kernel(
    xs, ys, zs,
    hidden_hbm, head_hbm, chosen_hbm, words,
    hid, weights, acc, stage_a, stage_b, outgoing, incoming, chosen_ref,
    load_sem, wsend, wrecv, ssend, srecv, gsend, grecv, near_sem, wide_sem, side_sem, line_sem,
):
    fidx = lax.axis_index("frames")
    cidx = lax.axis_index("codes")
    x, core = fidx // 2, fidx % 2
    y, z = cidx // zs, cidx % zs
    q, quad = z % 4, z // 4
    level = y * (zs // 4) + quad
    sib = 1 - core
    xl, xr, xo = (x + xs - 1) % xs, (x + 1) % xs, (x + 2) % xs

    def at(px, pcore, py, pz):
        return (px * 2 + pcore, py * zs + pz)

    mark("p00issue")
    own_head = pltpu.make_async_copy(head_hbm, weights.at[fidx], load_sem.at[0])
    own_head.start()
    chosen_load = pltpu.make_async_copy(chosen_hbm, chosen_ref, load_sem.at[5])
    quarter = hid.shape[0] // 4
    loads = []
    for i in range(4):
        rows = pl.ds(i * quarter, quarter)
        copy = pltpu.make_async_copy(hidden_hbm.at[rows], hid.at[rows], load_sem.at[1 + i])
        copy.start()
        loads.append(copy)

    mark("p01barrier")
    mate = at(x, sib, y, z)
    left, right = at(xl, core, y, z), at(xr, core, y, z)
    z_near = [at(x, core, y, (z + d) % zs) for d in (1, zs - 1)]
    z_wide = [at(x, core, y, (z + d) % zs) for d in (2, zs - 2)]
    y_near = [at(x, core, (y + d) % ys, z) for d in (1, ys - 1)]
    barrier = pltpu.get_barrier_semaphore()
    around = [mate, left, right, at(xo, core, y, z)] + z_near + y_near
    for peer in around:
        pl.semaphore_signal(barrier, inc=1, device_id=peer, device_id_type=MESH)
    chosen_load.start()
    pl.semaphore_wait(barrier, len(around))
    for peer in z_near:
        pl.semaphore_signal(near_sem, inc=1, device_id=peer, device_id_type=MESH)
    for peer in y_near:
        pl.semaphore_signal(side_sem, inc=1, device_id=peer, device_id_type=MESH)
    own_head.wait()

    mark("p02gather")
    half = weights.shape[1] // 2

    def piece(slot, part):
        if part is None:
            return weights.at[slot]
        return weights.at[slot, pl.ds(part * half, half)]

    def push(slot, part, index, peer):
        copy = pltpu.make_async_remote_copy(
            src_ref=piece(slot, part), dst_ref=piece(slot, part),
            send_sem=wsend, recv_sem=wrecv.at[index],
            device_id=peer, device_id_type=MESH,
        )
        copy.start()

    def landed(slot, part, index):
        pltpu.make_async_remote_copy(
            src_ref=piece(slot, part), dst_ref=piece(slot, part),
            send_sem=wsend, recv_sem=wrecv.at[index],
            device_id=at(x, sib, y, z), device_id_type=MESH,
        ).wait_recv()

    push(fidx, None, 0, mate)
    push(fidx, None, 1, right)
    push(fidx, None, 2, left)
    push(fidx, None, 3, at(xo, core, y, z))
    pl.semaphore_wait(near_sem, 2)
    for peer in z_wide:
        pl.semaphore_signal(wide_sem, inc=1, device_id=peer, device_id_type=MESH)
    left_slot, right_slot, far_slot = xl * 2 + core, xr * 2 + core, xo * 2 + core
    depth = 2 * weights.shape[1]

    def product(rows, chip):
        pair = weights[pl.ds(chip * 2, 2)].reshape(depth, weights.shape[2])
        cols = pl.ds(pl.multiple_of(chip * depth, depth), depth)
        return jnp.dot(hid[rows, cols], pair, preferred_element_type=jnp.float32)

    mark("p03ownmm")
    landed(x * 2 + sib, None, 0)
    step = 512
    for i in range(4):
        loads[i].wait()
        for j in range(quarter // step):
            rows = pl.ds(i * quarter + j * step, step)
            acc[rows] = product(rows, x)
    mark("p04relay")
    landed(left_slot, None, 1)
    push(left_slot, None, 4, mate)
    landed(right_slot, None, 2)
    push(right_slot, None, 5, mate)
    landed(far_slot, None, 3)
    push(far_slot, None, 6, mate)
    mark("p05sidemm")
    landed(xl * 2 + sib, None, 4)
    for i in range(hid.shape[0] // step):
        rows = pl.ds(i * step, step)
        acc[rows] += product(rows, xl)
    mark("p06farwait")
    landed(xr * 2 + sib, None, 5)
    landed(xo * 2 + sib, None, 6)
    mark("p07stats")
    pl.semaphore_wait(wide_sem, 2)
    pl.semaphore_wait(side_sem, 2)
    for d in range(1, ys):
        pl.semaphore_signal(line_sem, inc=1, device_id=at(x, core, (y + d) % ys, z), device_id_type=MESH)
    chosen_load.wait()
    offset = q * weights.shape[2]
    low = q < 2
    order = [jnp.where(low, 3, 0), jnp.where(low, 2, 1)]
    order.append(jnp.where(low, jnp.where(q == 1, 0, 1), jnp.where(q == 2, 3, 2)))
    order.append(q)
    stages = (stage_a, stage_b)

    def rows_of(s, t):
        return pl.ds(pl.multiple_of(order[s] * quarter + t * BLOCK, BLOCK), BLOCK)

    def prepare(s, t):
        rows = rows_of(s, t)
        stages[s % 2][pl.ds(t * BLOCK, BLOCK)] = (acc[rows] + (product(rows, xr) + product(rows, xo))) * LOG2E

    blocks = quarter // BLOCK
    for t in range(blocks):
        prepare(0, t)
    for s in range(4):
        part = order[s]
        for t in range(blocks):
            if s < 3:
                prepare(s + 1, t)
            wanted = chosen_ref[pl.ds(level, 1), rows_of(s, t)] - offset
            for i in range(BLOCK // TILE):
                row = t * (BLOCK // TILE) + i
                scaled = stages[s % 2][pl.ds(row * TILE, TILE)]
                stats = tile_stats(scaled, wanted[:, i * TILE:(i + 1) * TILE])
                for k in range(4):
                    outgoing[part, k, pl.ds(row, 1), :] = stats[k]
        if s < 3:
            copy = pltpu.make_async_remote_copy(
                src_ref=outgoing.at[part], dst_ref=incoming.at[q],
                send_sem=ssend, recv_sem=srecv,
                device_id=at(x, core, y, quad * 4 + part), device_id_type=MESH,
            )
            copy.start()

    mark("p08statwait")
    found = [tuple(outgoing[q, k] for k in range(4))]
    stat_sets = pltpu.make_async_remote_copy(
        src_ref=outgoing.at[pl.ds(0, 3)], dst_ref=incoming.at[pl.ds(0, 3)],
        send_sem=ssend, recv_sem=srecv, device_id=mate, device_id_type=MESH,
    )
    stat_sets.wait_recv()
    for s in range(3):
        found.append(tuple(incoming[order[s], k] for k in range(4)))
    top = functools.reduce(jnp.maximum, [f[0] for f in found])
    total = weighted = picked = jnp.zeros_like(top)
    for own_top, own_total, own_weighted, own_picked in found:
        gap = own_top - top
        factor = jnp.exp2(gap)
        total += factor * own_total
        weighted += factor * (own_weighted + gap * own_total)
        picked += own_picked
    bits = jnp.log(total)
    confidence = (picked - top) * LN2 - bits
    entropy = bits - LN2 * (weighted / total)
    words[cidx] = lax.shift_left(encode(-confidence, CONF_CODE), 16) | encode(entropy, ENT_CODE)

    mark("p09spread")
    pl.semaphore_wait(line_sem, ys - 1)
    for dz in (4, 3, zs - 3, 2, zs - 2, 1, zs - 1, 0):
        for dy in (2, 1, ys - 1, 0):
            if dz or dy:
                pltpu.make_async_remote_copy(
                    src_ref=words.at[cidx], dst_ref=words.at[cidx],
                    send_sem=gsend, recv_sem=grecv,
                    device_id=at(x, core, (y + dy) % ys, (z + dz) % zs), device_id_type=MESH,
                ).start()
    rest = words.at[pl.ds(0, ys * zs - 1)]
    finals = pltpu.make_async_remote_copy(
        src_ref=rest, dst_ref=rest, send_sem=gsend, recv_sem=grecv, device_id=mate, device_id_type=MESH,
    )
    finals.wait_recv()

    mark("p11drain")
    pltpu.make_async_remote_copy(
        src_ref=weights.at[pl.ds(0, PUSHES)], dst_ref=weights.at[pl.ds(0, PUSHES)],
        send_sem=wsend, recv_sem=wrecv.at[0], device_id=mate, device_id_type=MESH,
    ).wait_send()
    stat_sets.wait_send()
    finals.wait_send()
    mark(None)


def encode(value, code):
    scale, largest = code
    steps = 65535 / math.log1p(largest * scale)
    level = jnp.log(1.0 + jnp.maximum(value, 0.0) * scale) * steps
    return jnp.minimum(level + 0.5, 65535.0).astype(jnp.int32)


def decode(number, code):
    scale, largest = code
    steps = 65535 / math.log1p(largest * scale)
    return (jnp.exp2(number.astype(jnp.float32) * (LOG2E / steps)) - 1.0) * (1 / scale)


def lay_out(words, conf_hbm, ent_hbm, conf, ent, sems):
    levels, rows = conf.shape
    copies = []
    for k, (out, dst) in enumerate(((conf, conf_hbm), (ent, ent_hbm))):
        for part in range(4):
            values = []
            for g in range(levels):
                word = words[g * 4 + part]
                if k == 0:
                    values.append(-decode(lax.shift_right_logical(word, 16), CONF_CODE))
                else:
                    values.append(decode(word & 65535, ENT_CODE))
            for j in range(rows // 4 // LANES):
                cols = pl.ds(part * (rows // 4) + j * LANES, LANES)
                out[:, cols] = jnp.concatenate([v[j:j + 1] for v in values], axis=0)
        copy = pltpu.make_async_copy(out, dst, sems.at[k])
        copy.start()
        copies.append(copy)
    for copy in copies:
        copy.wait()


def on_device(xs, ys, zs, hidden, head, chosen):
    rows, width = hidden.shape
    depth, columns = head.shape
    levels = chosen.shape[0]
    quarter = rows // 4
    dma = pltpu.SemaphoreType.DMA
    out = jax.ShapeDtypeStruct((levels, rows), jnp.float32)
    vmem = pl.BlockSpec(memory_space=pltpu.VMEM)
    anywhere = pl.BlockSpec(memory_space=pltpu.HBM)
    words = pl.pallas_call(
        functools.partial(kernel, xs, ys, zs),
        out_shape=pltpu.VMEM((ys * zs, quarter // LANES, LANES), jnp.int32),
        in_specs=[anywhere, anywhere, anywhere],
        out_specs=vmem,
        scratch_shapes=[
            pltpu.VMEM((rows, width), jnp.bfloat16),
            pltpu.VMEM((width // depth, depth, columns), jnp.bfloat16),
            pltpu.VMEM((rows, columns), jnp.float32),
            pltpu.VMEM((quarter, columns), jnp.float32),
            pltpu.VMEM((quarter, columns), jnp.float32),
            pltpu.VMEM((4, 4, quarter // LANES, LANES), jnp.float32),
            pltpu.VMEM((4, 4, quarter // LANES, LANES), jnp.float32),
            pltpu.VMEM((levels, rows), jnp.int32),
            dma((6,)), dma(()), dma((7,)), dma(()), dma(()), dma(()), dma(()),
            pltpu.SemaphoreType.REGULAR, pltpu.SemaphoreType.REGULAR,
            pltpu.SemaphoreType.REGULAR, pltpu.SemaphoreType.REGULAR,
        ],
        compiler_params=pltpu.CompilerParams(collective_id=0, has_side_effects=True, vmem_limit_bytes=56 << 20),
    )(hidden, head, chosen)
    return pl.pallas_call(
        lay_out,
        out_shape=(out, out),
        in_specs=[vmem],
        out_specs=(anywhere, anywhere),
        scratch_shapes=[pltpu.VMEM((levels, rows), jnp.float32)] * 2 + [dma((2,))],
        compiler_params=pltpu.CompilerParams(vmem_limit_bytes=4 << 20),
    )(words)


def solution(mesh):
    return jax.shard_map(
        functools.partial(on_device, mesh.shape["frames"] // 2, 4, mesh.shape["codes"] // 4),
        mesh=mesh,
        in_specs=(P("frames", None), P("frames", "codes"), P(None, "frames")),
        out_specs=(P(None, "frames"), P(None, "frames")),
        check_vma=False,
    )
```

time: 29.5 us -> 26.9 us (0.912)
  Pallas kernels: 28.7 us -> 26 us
    pallas_call x1, Pallas kernels: 27.9 us -> 25.2 us  [on_device(): pl.pallas_call(functools.partial(kernel, xs, ys, zs), out_shape=pltpu.VME...]
where the time goes in v3:
time: 26.9 us; the launch traced here: 26.6 us
  Pallas kernels  26 us (97%)
  between operations  0.64 us (2%)
    pallas_call x1, Pallas kernels, on_device(): pl.pallas_call(functools.partial(kernel, xs, ys, zs), out_shape=pltpu.VME...  25.2 us
    pallas_call x1, Pallas kernels, on_device(): pl.pallas_call(lay_out, out_shape=(out, out), in_specs=[vmem], out_specs=...  0.85 us

profile of v3, /device:TPU:2, one launch (start us, length us, event | category | flops | bytes accessed | tf_op | source)
XLA Modules:
  0.0 26.6 jit_solution(10141023969459062542)
XLA Ops:
  0.6 25.2 %shard_map.50.words = s32[32,8,128]{2,1,0:T(8,128)S(1)} custom-call(bf16[4096,1024]{1,0:T(8,128)(2,1)} %hidden_hbm.1, bf16[128,256]{1,0:T(8,128)(2,1)} %head_hbm.1, s32[8,4096]{1,0:T(8,128)} %chosen_hbm.1), custom_call_target="tpu_custom_call" | custom-call | tf_op jit(solution)/shard_map/pallas_call | solution.py:303
  25.8 0.8 %shard_map.51 = (f32[8,4096]{1,0:T(8,128)}, f32[8,4096]{1,0:T(8,128)}) custom-call(s32[32,8,128]{2,1,0:T(8,128)S(1)} %shard_map.50.words), custom_call_target="tpu_custom_call" | custom-call | tf_op jit(solution)/shard_map/pallas_call | solution.py:323

commit v4 on v3

--- a/solution.py
+++ b/solution.py
@@ -64,20 +64,25 @@
 ):
     fidx = lax.axis_index("frames")
     cidx = lax.axis_index("codes")
-    x, core = fidx // 2, fidx % 2
-    y, z = cidx // zs, cidx % zs
-    q, quad = z % 4, z // 4
-    level = y * (zs // 4) + quad
+    own_head = pltpu.make_async_copy(head_hbm, weights.at[fidx], load_sem.at[0])
+    own_head.start()
+    x, core = lax.div(fidx, 2), lax.rem(fidx, 2)
+    y, z = lax.div(cidx, zs), lax.rem(cidx, zs)
     sib = 1 - core
-    xl, xr, xo = (x + xs - 1) % xs, (x + 1) % xs, (x + 2) % xs
+    xl, xr, xo = lax.rem(x + xs - 1, xs), lax.rem(x + 1, xs), lax.rem(x + 2, xs)
 
     def at(px, pcore, py, pz):
         return (px * 2 + pcore, py * zs + pz)
 
-    mark("p00issue")
-    own_head = pltpu.make_async_copy(head_hbm, weights.at[fidx], load_sem.at[0])
-    own_head.start()
-    chosen_load = pltpu.make_async_copy(chosen_hbm, chosen_ref, load_sem.at[5])
+    mark("p01barrier")
+    mate = at(x, sib, y, z)
+    left, right, far = at(xl, core, y, z), at(xr, core, y, z), at(xo, core, y, z)
+    barrier = pltpu.get_barrier_semaphore()
+    z_near = [at(x, core, y, lax.rem(z + d, zs)) for d in (1, zs - 1)]
+    y_near = [at(x, core, lax.rem(y + d, ys), z) for d in (1, ys - 1)]
+    around = [mate, left, right, far] + z_near + y_near
+    for peer in around:
+        pl.semaphore_signal(barrier, inc=1, device_id=peer, device_id_type=MESH)
     quarter = hid.shape[0] // 4
     loads = []
     for i in range(4):
@@ -85,17 +90,7 @@
         copy = pltpu.make_async_copy(hidden_hbm.at[rows], hid.at[rows], load_sem.at[1 + i])
         copy.start()
         loads.append(copy)
-
-    mark("p01barrier")
-    mate = at(x, sib, y, z)
-    left, right = at(xl, core, y, z), at(xr, core, y, z)
-    z_near = [at(x, core, y, (z + d) % zs) for d in (1, zs - 1)]
-    z_wide = [at(x, core, y, (z + d) % zs) for d in (2, zs - 2)]
-    y_near = [at(x, core, (y + d) % ys, z) for d in (1, ys - 1)]
-    barrier = pltpu.get_barrier_semaphore()
-    around = [mate, left, right, at(xo, core, y, z)] + z_near + y_near
-    for peer in around:
-        pl.semaphore_signal(barrier, inc=1, device_id=peer, device_id_type=MESH)
+    chosen_load = pltpu.make_async_copy(chosen_hbm, chosen_ref, load_sem.at[5])
     chosen_load.start()
     pl.semaphore_wait(barrier, len(around))
     for peer in z_near:
@@ -105,6 +100,11 @@
     own_head.wait()
 
     mark("p02gather")
+    y_at = [lax.rem(y + d, ys) for d in range(ys)]
+    z_at = [lax.rem(z + d, zs) for d in range(zs)]
+    q, quad = lax.rem(z, 4), lax.div(z, 4)
+    level = y * (zs // 4) + quad
+    z_wide = [at(x, core, y, z_at[d]) for d in (2, zs - 2)]
     half = weights.shape[1] // 2
 
     def piece(slot, part):
@@ -130,7 +130,7 @@
     push(fidx, None, 0, mate)
     push(fidx, None, 1, right)
     push(fidx, None, 2, left)
-    push(fidx, None, 3, at(xo, core, y, z))
+    push(fidx, None, 3, far)
     pl.semaphore_wait(near_sem, 2)
     for peer in z_wide:
         pl.semaphore_signal(wide_sem, inc=1, device_id=peer, device_id_type=MESH)
@@ -169,7 +169,7 @@
     pl.semaphore_wait(wide_sem, 2)
     pl.semaphore_wait(side_sem, 2)
     for d in range(1, ys):
-        pl.semaphore_signal(line_sem, inc=1, device_id=at(x, core, (y + d) % ys, z), device_id_type=MESH)
+        pl.semaphore_signal(line_sem, inc=1, device_id=at(x, core, y_at[d], z), device_id_type=MESH)
     chosen_load.wait()
     offset = q * weights.shape[2]
     low = q < 2
@@ -238,7 +238,7 @@
                 pltpu.make_async_remote_copy(
                     src_ref=words.at[cidx], dst_ref=words.at[cidx],
                     send_sem=gsend, recv_sem=grecv,
-                    device_id=at(x, core, (y + dy) % ys, (z + dz) % zs), device_id_type=MESH,
+                    device_id=at(x, core, y_at[dy], z_at[dz]), device_id_type=MESH,
                 ).start()
     rest = words.at[pl.ds(0, ys * zs - 1)]
     finals = pltpu.make_async_remote_copy(
@@ -271,22 +271,22 @@
 
 def lay_out(words, conf_hbm, ent_hbm, conf, ent, sems):
     levels, rows = conf.shape
+    quarter = rows // 4
     copies = []
-    for k, (out, dst) in enumerate(((conf, conf_hbm), (ent, ent_hbm))):
-        for part in range(4):
-            values = []
-            for g in range(levels):
-                word = words[g * 4 + part]
-                if k == 0:
-                    values.append(-decode(lax.shift_right_logical(word, 16), CONF_CODE))
-                else:
-                    values.append(decode(word & 65535, ENT_CODE))
-            for j in range(rows // 4 // LANES):
-                cols = pl.ds(part * (rows // 4) + j * LANES, LANES)
+    for part in range(4):
+        found = [words[g * 4 + part] for g in range(levels)]
+        fields = (
+            (conf, conf_hbm, [-decode(lax.shift_right_logical(w, 16), CONF_CODE) for w in found]),
+            (ent, ent_hbm, [decode(w & 65535, ENT_CODE) for w in found]),
+        )
+        for k, (out, dst, values) in enumerate(fields):
+            for j in range(quarter // LANES):
+                cols = pl.ds(part * quarter + j * LANES, LANES)
                 out[:, cols] = jnp.concatenate([v[j:j + 1] for v in values], axis=0)
-        copy = pltpu.make_async_copy(out, dst, sems.at[k])
-        copy.start()
-        copies.append(copy)
+            span = pl.ds(part * quarter, quarter)
+            copy = pltpu.make_async_copy(out.at[:, span], dst.at[:, span], sems.at[2 * part + k])
+            copy.start()
+            copies.append(copy)
     for copy in copies:
         copy.wait()
 
@@ -325,7 +325,7 @@
         out_shape=(out, out),
         in_specs=[vmem],
         out_specs=(anywhere, anywhere),
-        scratch_shapes=[pltpu.VMEM((levels, rows), jnp.float32)] * 2 + [dma((2,))],
+        scratch_shapes=[pltpu.VMEM((levels, rows), jnp.float32)] * 2 + [dma((8,))],
         compiler_params=pltpu.CompilerParams(vmem_limit_bytes=4 << 20),
     )(words)
 

time: 26.9 us -> 26.9 us (level)
  no operation moved by 1% of the time
where the time goes in v4:
time: 26.9 us; the launch traced here: 26.6 us
  Pallas kernels  26 us (97%)
  between operations  0.64 us (2%)
    pallas_call x1, Pallas kernels, on_device(): pl.pallas_call(functools.partial(kernel, xs, ys, zs), out_shape=pltpu.VME...  25.1 us
    pallas_call x1, Pallas kernels, on_device(): pl.pallas_call(lay_out, out_shape=(out, out), in_specs=[vmem], out_specs=...  0.86 us

profile of v4, /device:TPU:2, one launch (start us, length us, event | category | flops | bytes accessed | tf_op | source)
XLA Modules:
  0.0 26.6 jit_solution(6554467141000648907)
XLA Ops:
  0.6 25.1 %shard_map.50.words = s32[32,8,128]{2,1,0:T(8,128)S(1)} custom-call(bf16[4096,1024]{1,0:T(8,128)(2,1)} %hidden_hbm.1, bf16[128,256]{1,0:T(8,128)(2,1)} %head_hbm.1, s32[8,4096]{1,0:T(8,128)} %chosen_hbm.1), custom_call_target="tpu_custom_call" | custom-call | tf_op jit(solution)/shard_map/pallas_call | solution.py:303
  25.7 0.9 %shard_map.51 = (f32[8,4096]{1,0:T(8,128)}, f32[8,4096]{1,0:T(8,128)}) custom-call(s32[32,8,128]{2,1,0:T(8,128)S(1)} %shard_map.50.words), custom_call_target="tpu_custom_call" | custom-call | tf_op jit(solution)/shard_map/pallas_call | solution.py:323

commit v5 on v4

--- a/solution.py
+++ b/solution.py
@@ -16,6 +16,8 @@
 TILE = 128
 BLOCK = 256
 PUSHES = 7
+LEAD = 3
+STEP = 1024
 CONF_CODE = (64.0, 20500.0)
 ENT_CODE = (1024.0, 6.95)
 PROFILE = False
@@ -144,7 +146,7 @@
 
     mark("p03ownmm")
     landed(x * 2 + sib, None, 0)
-    step = 512
+    step = STEP
     for i in range(4):
         loads[i].wait()
         for j in range(quarter // step):
@@ -186,13 +188,14 @@
         stages[s % 2][pl.ds(t * BLOCK, BLOCK)] = (acc[rows] + (product(rows, xr) + product(rows, xo))) * LOG2E
 
     blocks = quarter // BLOCK
-    for t in range(blocks):
+    for t in range(LEAD):
         prepare(0, t)
     for s in range(4):
         part = order[s]
         for t in range(blocks):
-            if s < 3:
-                prepare(s + 1, t)
+            ahead = s * blocks + t + LEAD
+            if ahead < 4 * blocks:
+                prepare(ahead // blocks, ahead % blocks)
             wanted = chosen_ref[pl.ds(level, 1), rows_of(s, t)] - offset
             for i in range(BLOCK // TILE):
                 row = t * (BLOCK // TILE) + i

time: 26.9 us -> 26.9 us (level)
  no operation moved by 1% of the time
where the time goes in v5:
time: 26.9 us; the launch traced here: 26.6 us
  Pallas kernels  25.9 us (96%)
  between operations  0.64 us (2%)
    pallas_call x1, Pallas kernels, on_device(): pl.pallas_call(functools.partial(kernel, xs, ys, zs), out_shape=pltpu.VME...  25.1 us
    pallas_call x1, Pallas kernels, on_device(): pl.pallas_call(lay_out, out_shape=(out, out), in_specs=[vmem], out_specs=...  0.86 us

profile of v5, /device:TPU:2, one launch (start us, length us, event | category | flops | bytes accessed | tf_op | source)
XLA Modules:
  0.0 26.6 jit_solution(2565070629745897843)
XLA Ops:
  0.6 25.1 %shard_map.50.words = s32[32,8,128]{2,1,0:T(8,128)S(1)} custom-call(bf16[4096,1024]{1,0:T(8,128)(2,1)} %hidden_hbm.1, bf16[128,256]{1,0:T(8,128)(2,1)} %head_hbm.1, s32[8,4096]{1,0:T(8,128)} %chosen_hbm.1), custom_call_target="tpu_custom_call" | custom-call | tf_op jit(solution)/shard_map/pallas_call | solution.py:306
  25.7 0.9 %shard_map.51 = (f32[8,4096]{1,0:T(8,128)}, f32[8,4096]{1,0:T(8,128)}) custom-call(s32[32,8,128]{2,1,0:T(8,128)S(1)} %shard_map.50.words), custom_call_target="tpu_custom_call" | custom-call | tf_op jit(solution)/shard_map/pallas_call | solution.py:326

commit v6 on v4

--- a/solution.py
+++ b/solution.py
@@ -84,13 +84,11 @@
     for peer in around:
         pl.semaphore_signal(barrier, inc=1, device_id=peer, device_id_type=MESH)
     quarter = hid.shape[0] // 4
-    loads = []
     for i in range(4):
         rows = pl.ds(i * quarter, quarter)
-        copy = pltpu.make_async_copy(hidden_hbm.at[rows], hid.at[rows], load_sem.at[1 + i])
+        copy = pltpu.make_async_copy(hidden_hbm.at[rows], hid.at[rows], load_sem.at[1])
         copy.start()
-        loads.append(copy)
-    chosen_load = pltpu.make_async_copy(chosen_hbm, chosen_ref, load_sem.at[5])
+    chosen_load = pltpu.make_async_copy(chosen_hbm, chosen_ref, load_sem.at[2])
     chosen_load.start()
     pl.semaphore_wait(barrier, len(around))
     for peer in z_near:
@@ -145,8 +143,8 @@
     mark("p03ownmm")
     landed(x * 2 + sib, None, 0)
     step = 512
+    pltpu.make_async_copy(hidden_hbm, hid, load_sem.at[1]).wait()
     for i in range(4):
-        loads[i].wait()
         for j in range(quarter // step):
             rows = pl.ds(i * quarter + j * step, step)
             acc[rows] = product(rows, x)
@@ -314,7 +312,7 @@
             pltpu.VMEM((4, 4, quarter // LANES, LANES), jnp.float32),
             pltpu.VMEM((4, 4, quarter // LANES, LANES), jnp.float32),
             pltpu.VMEM((levels, rows), jnp.int32),
-            dma((6,)), dma(()), dma((7,)), dma(()), dma(()), dma(()), dma(()),
+            dma((3,)), dma(()), dma((7,)), dma(()), dma(()), dma(()), dma(()),
             pltpu.SemaphoreType.REGULAR, pltpu.SemaphoreType.REGULAR,
             pltpu.SemaphoreType.REGULAR, pltpu.SemaphoreType.REGULAR,
         ],

time: 26.9 us -> 26.8 us (level)
  no operation moved by 1% of the time
where the time goes in v6:
time: 26.8 us; the launch traced here: 26.6 us
  Pallas kernels  25.9 us (97%)
  between operations  0.64 us (2%)
    pallas_call x1, Pallas kernels, on_device(): pl.pallas_call(functools.partial(kernel, xs, ys, zs), out_shape=pltpu.VME...  25.1 us
    pallas_call x1, Pallas kernels, on_device(): pl.pallas_call(lay_out, out_shape=(out, out), in_specs=[vmem], out_specs=...  0.86 us

profile of v6, /device:TPU:2, one launch (start us, length us, event | category | flops | bytes accessed | tf_op | source)
XLA Modules:
  0.0 26.6 jit_solution(16507336965357784349)
XLA Ops:
  0.6 25.1 %shard_map.50.words = s32[32,8,128]{2,1,0:T(8,128)S(1)} custom-call(bf16[4096,1024]{1,0:T(8,128)(2,1)} %hidden_hbm.1, bf16[128,256]{1,0:T(8,128)(2,1)} %head_hbm.1, s32[8,4096]{1,0:T(8,128)} %chosen_hbm.1), custom_call_target="tpu_custom_call" | custom-call | tf_op jit(solution)/shard_map/pallas_call | solution.py:301
  25.7 0.9 %shard_map.51 = (f32[8,4096]{1,0:T(8,128)}, f32[8,4096]{1,0:T(8,128)}) custom-call(s32[32,8,128]{2,1,0:T(8,128)S(1)} %shard_map.50.words), custom_call_target="tpu_custom_call" | custom-call | tf_op jit(solution)/shard_map/pallas_call | solution.py:321

commit v7 on v6

--- a/solution.py
+++ b/solution.py
@@ -80,7 +80,7 @@
     barrier = pltpu.get_barrier_semaphore()
     z_near = [at(x, core, y, lax.rem(z + d, zs)) for d in (1, zs - 1)]
     y_near = [at(x, core, lax.rem(y + d, ys), z) for d in (1, ys - 1)]
-    around = [mate, left, right, far] + z_near + y_near
+    around = [far] + z_near + y_near + [left, right, mate]
     for peer in around:
         pl.semaphore_signal(barrier, inc=1, device_id=peer, device_id_type=MESH)
     quarter = hid.shape[0] // 4

time: 26.8 us -> 26.8 us (level)
  no operation moved by 1% of the time
where the time goes in v7:
time: 26.8 us; the launch traced here: 26.5 us
  Pallas kernels  25.8 us (96%)
  between operations  0.64 us (2%)
    pallas_call x1, Pallas kernels, on_device(): pl.pallas_call(functools.partial(kernel, xs, ys, zs), out_shape=pltpu.VME...  25 us
    pallas_call x1, Pallas kernels, on_device(): pl.pallas_call(lay_out, out_shape=(out, out), in_specs=[vmem], out_specs=...  0.86 us

profile of v7, /device:TPU:2, one launch (start us, length us, event | category | flops | bytes accessed | tf_op | source)
XLA Modules:
  0.0 26.5 jit_solution(1004998325009441058)
XLA Ops:
  0.6 25.0 %shard_map.50.words = s32[32,8,128]{2,1,0:T(8,128)S(1)} custom-call(bf16[4096,1024]{1,0:T(8,128)(2,1)} %hidden_hbm.1, bf16[128,256]{1,0:T(8,128)(2,1)} %head_hbm.1, s32[8,4096]{1,0:T(8,128)} %chosen_hbm.1), custom_call_target="tpu_custom_call" | custom-call | tf_op jit(solution)/shard_map/pallas_call | solution.py:301
  25.6 0.9 %shard_map.51 = (f32[8,4096]{1,0:T(8,128)}, f32[8,4096]{1,0:T(8,128)}) custom-call(s32[32,8,128]{2,1,0:T(8,128)S(1)} %shard_map.50.words), custom_call_target="tpu_custom_call" | custom-call | tf_op jit(solution)/shard_map/pallas_call | solution.py:321
